TPU v7x, 32 devices: a whole 2x2x4 slice. The times are simulated.
32 devices in a mesh: fsdp: 16 (over z, y, core), tp: 2 (over x).
Axes of the slice: x: 2, y: 2, z: 4, core: 2. Of those that a mesh axis runs over, the one named last changes fastest.
Arguments:
- hidden: bfloat16 [32, 5120], P(None, 'fsdp'), may hold values from -20 to 20
- query_weight: bfloat16 [5120, 5120], P(None, ('tp', 'fsdp')), may hold values from -0.078125 to 0.078125
- key_weight: bfloat16 [5120, 1024], P(None, ('tp', 'fsdp')), may hold values from -0.078125 to 0.078125
- value_weight: bfloat16 [5120, 1024], P(None, ('tp', 'fsdp')), may hold values from -0.078125 to 0.078125
- output_weight: bfloat16 [5120, 5120], P(('tp', 'fsdp')), may hold values from -0.078125 to 0.078125
- gate_weight: bfloat16 [5120, 27648], P(None, ('tp', 'fsdp')), may hold values from -0.078125 to 0.078125
- up_weight: bfloat16 [5120, 27648], P(None, ('tp', 'fsdp')), may hold values from -0.078125 to 0.078125
- down_weight: bfloat16 [27648, 5120], P(('tp', 'fsdp')), may hold values from -0.0390625 to 0.0390625
- history: float32 [7, 1024], replicated, may hold values from 0.0001 to 1, as said below
- slot: int32 [1], replicated, may hold values from 0 to 1023
- lengths: int32 [32], P('fsdp'), may hold values from 512 to 4096, as said below
- key_cache: bfloat16 [32, 4096, 1024], P('fsdp', None, 'tp'), may hold values from -1000 to 1000
- value_cache: bfloat16 [32, 4096, 1024], P('fsdp', None, 'tp'), may hold values from -6 to 6
Outputs:
- attention_out: bfloat16 [32, 5120], P('fsdp', 'tp')
- query_rollout: bfloat16 [5120, 5120], P('fsdp', 'tp')
- key_rollout: bfloat16 [5120, 1024], P('fsdp', 'tp')
- value_rollout: bfloat16 [5120, 1024], P('fsdp', 'tp')
- output_rollout: bfloat16 [5120, 5120], P('tp', 'fsdp')
- gate_rollout: bfloat16 [5120, 27648], P('fsdp', 'tp')
- up_rollout: bfloat16 [5120, 27648], P('fsdp', 'tp')
- down_rollout: bfloat16 [27648, 5120], P('tp', 'fsdp')
- new_history: float32 [7, 1024], replicated
Inputs may be any that keep to these rules, and one draw needn't show every extreme that they name: `history`: strictly positive. `lengths`: some sequence has all 4096 slots valid.
All inputs are finite; a program needn't handle non-finite values.
Results may differ from a plain program's by a relative error of at most 0.012.
The roundings to bfloat16 on the way count: a program that leaves them out, or rounds other values in their place, can miss the bound.
Values may be sent and summed in bfloat16 or wider, within the bound.
A program may use at most 192 MiB of HBM per device.

v0:
```python
import jax
import jax.numpy as jnp
from jax import lax
from jax.sharding import PartitionSpec as P

D = 5120
HEADS = 40
KV_HEADS = 8
HEAD_DIM = 128


target_peak = 4.0
norm_eps = 1e-06
rope_theta = 1000000.0


def largest(tensor):
    return jnp.max(jnp.abs(tensor.astype(jnp.float32)))


def scaling(peaks, history, slot):
    marked = lax.broadcasted_iota(jnp.int32, history.shape, 1) == slot[0]
    kept = jnp.max(jnp.where(marked, jnp.zeros_like(history), history), axis=1)
    return (target_peak / jnp.maximum(peaks, kept), jnp.where(marked, peaks[:, None], history))


def quantize(tensor, factor):
    return (tensor.astype(jnp.float32) * factor).astype(jnp.bfloat16)


def rotate(vectors, positions):
    half_dim = vectors.shape[-1] // 2
    ladder = jnp.arange(half_dim, dtype=jnp.float32)
    spread = rope_theta ** (-2.0 * ladder / vectors.shape[-1])
    angle = positions.astype(jnp.float32)[:, None] * spread[None, :]
    cosine = jnp.cos(angle)[:, None, :]
    sine = jnp.sin(angle)[:, None, :]
    first = vectors[..., :half_dim]
    second = vectors[..., half_dim:]
    return jnp.concatenate(
        [first * cosine - second * sine, second * cosine + first * sine], axis=-1
    )


def regroup(query_part, key_part, value_part, output_part, gate_part, up_part, down_part):
    columns = (
        lax.all_to_all(query_part, "fsdp", split_axis=0, concat_axis=1, tiled=True),
        lax.all_to_all(key_part, "fsdp", split_axis=0, concat_axis=1, tiled=True),
        lax.all_to_all(value_part, "fsdp", split_axis=0, concat_axis=1, tiled=True),
        lax.all_to_all(gate_part, "fsdp", split_axis=0, concat_axis=1, tiled=True),
        lax.all_to_all(up_part, "fsdp", split_axis=0, concat_axis=1, tiled=True),
    )
    rowwise = (
        lax.all_to_all(output_part, "fsdp", split_axis=1, concat_axis=0, tiled=True),
        lax.all_to_all(down_part, "fsdp", split_axis=1, concat_axis=0, tiled=True),
    )
    return (columns[0], columns[1], columns[2], rowwise[0], columns[3], columns[4], rowwise[1])


def attend(query, key_new, value_new, key_cache, value_cache, lengths):
    count_seq = query.shape[0]
    kv_count = query.shape[1]
    head_dim = query.shape[3]
    cache_len = key_cache.shape[1]
    keys = key_cache.reshape(count_seq, cache_len, kv_count, head_dim)
    values = value_cache.reshape(count_seq, cache_len, kv_count, head_dim)
    scale = head_dim ** (-0.5)
    scores = jnp.einsum("bkgd,bjkd->bkgj", query, keys, preferred_element_type=jnp.float32) * scale
    own = (
        jnp.sum(query.astype(jnp.float32) * key_new.astype(jnp.float32)[:, :, None, :], axis=-1)
        * scale
    )
    valid = (lax.broadcasted_iota(jnp.int32, (count_seq, cache_len), 1) < lengths[:, None])[
        :, None, None, :
    ]
    top = jnp.maximum(jnp.max(jnp.where(valid, scores, -1e30), axis=-1), own)
    weights = jnp.where(valid, jnp.exp(scores - top[..., None]), 0.0)
    own_weight = jnp.exp(own - top)
    total = jnp.sum(weights, axis=-1) + own_weight
    probs = (weights / total[..., None]).astype(jnp.bfloat16)
    own_prob = (own_weight / total).astype(jnp.bfloat16)
    mixed = jnp.einsum("bkgj,bjkd->bkgd", probs, values, preferred_element_type=jnp.float32)
    mixed = (
        mixed
        + own_prob.astype(jnp.float32)[..., None] * value_new.astype(jnp.float32)[:, :, None, :]
    )
    return mixed.astype(jnp.bfloat16).reshape(count_seq, -1)


def per_device(
    hidden,
    query_weight,
    key_weight,
    value_weight,
    output_weight,
    gate_weight,
    up_weight,
    down_weight,
    history,
    slot,
    lengths,
    key_cache,
    value_cache,
):
    trainer = (
        query_weight,
        key_weight,
        value_weight,
        output_weight,
        gate_weight,
        up_weight,
        down_weight,
    )
    peaks = jnp.stack([lax.pmax(largest(tensor), ("fsdp", "tp")) for tensor in trainer])
    factors, new_history = scaling(peaks, history, slot)
    arrived = regroup(
        query_weight, key_weight, value_weight, output_weight, gate_weight, up_weight, down_weight
    )
    rollout = tuple((quantize(arrived[number], factors[number]) for number in range(7)))
    (
        query_rollout,
        key_rollout,
        value_rollout,
        output_rollout,
        gate_rollout,
        up_rollout,
        down_rollout,
    ) = rollout
    widened = hidden.astype(jnp.float32)
    squares = jnp.sum(widened * widened, axis=1)
    joined = jnp.concatenate([query_rollout, key_rollout, value_rollout], axis=1)
    partial_value = jnp.dot(hidden, joined, preferred_element_type=jnp.float32)
    summed, total_sq = (
        lax.psum_scatter(partial_value, "fsdp", scatter_dimension=0, tiled=True),
        lax.psum_scatter(squares, "fsdp", scatter_dimension=0, tiled=True),
    )
    inv_rms = lax.rsqrt(total_sq / D + norm_eps)[:, None]
    width_q = query_rollout.shape[1]
    width_k = key_rollout.shape[1]
    query = summed[:, :width_q] * inv_rms / factors[0]
    key_new = summed[:, width_q : width_q + width_k] * inv_rms / factors[1]
    value_new = summed[:, width_q + width_k :] * inv_rms / factors[2]
    count_seq = summed.shape[0]
    query = rotate(query.reshape(count_seq, -1, HEAD_DIM), lengths).astype(jnp.bfloat16)
    query = query.reshape(count_seq, -1, HEADS // KV_HEADS, HEAD_DIM)
    key_new = rotate(key_new.reshape(count_seq, -1, HEAD_DIM), lengths).astype(jnp.bfloat16)
    value_new = value_new.reshape(count_seq, -1, HEAD_DIM).astype(jnp.bfloat16)
    attention_out = attend(query, key_new, value_new, key_cache, value_cache, lengths)
    return (
        attention_out,
        query_rollout,
        key_rollout,
        value_rollout,
        output_rollout,
        gate_rollout,
        up_rollout,
        down_rollout,
        new_history,
    )


def solution(mesh):
    return jax.shard_map(
        per_device,
        mesh=mesh,
        in_specs=(
            P(None, "fsdp"),
            P(None, ("tp", "fsdp")),
            P(None, ("tp", "fsdp")),
            P(None, ("tp", "fsdp")),
            P(("tp", "fsdp"), None),
            P(None, ("tp", "fsdp")),
            P(None, ("tp", "fsdp")),
            P(("tp", "fsdp"), None),
            P(),
            P(),
            P("fsdp"),
            P("fsdp", None, "tp"),
            P("fsdp", None, "tp"),
        ),
        out_specs=(
            P("fsdp", "tp"),
            P("fsdp", "tp"),
            P("fsdp", "tp"),
            P("fsdp", "tp"),
            P("tp", "fsdp"),
            P("fsdp", "tp"),
            P("fsdp", "tp"),
            P("tp", "fsdp"),
            P(),
        ),
        check_vma=False,
    )
```

profile of v0, /device:TPU:0, one launch (start us, length us, event | category | flops | bytes accessed | tf_op | source)
XLA Modules:
  0.0 1055.8 jit_solution(7451371705270785353)
XLA Ops:
  7.2 1.3 all_to_all.72
  9.3 7.4 all-to-all-start.1
  18.9 10.0 all-to-all-done.1
  29.6 3.6 all-to-all-start.2
  33.2 3.3 all_to_all.70
  36.5 1.7 copy.68
  38.2 7.1 all-to-all-done.2
  45.3 4.4 all-to-all-start
  49.8 3.3 all_to_all.76
  53.1 1.7 copy.77
  54.8 33.7 %all-to-all-done = bf16[16,320,160]{1,2,0:T(8,128)(2,1)} async-done(((bf16[16,320,160]{1,2,0:T(8,128)(2,1)}), bf16[16,320,160]{1,2,0:T(8,128)(2,1)}, u32[]{:S(2)}, u32[]{:S(2)}) %all-to-all-start) | async-done | bytes 1638432 | tf_op jit(solution)/shard_map/all_to_all | solution.py:47
  88.4 10.7 %all-to-all-start.3 = ((bf16[160,16,320]{2,0,1:T(8,128)(2,1)}), bf16[160,16,320]{2,0,1:T(8,128)(2,1)S(1)}, u32[]{:S(2)}, u32[]{:S(2)}) async-start(bf16[160,16,320]{2,0,1:T(8,128)(2,1)} %copy.77), calls=%async_computation.3 | async-start | bytes 3932160 | tf_op jit(solution)/shard_map/all_to_all | solution.py:54
  99.1 12.7 %copy.78 = bf16[5120,864]{1,0:T(8,128)(2,1)} copy(bf16[5120,864]{0,1:T(8,128)(2,1)} %param.18) | data formatting | bytes 17694720 | tf_op args[5]
  111.8 26.0 %all-to-all-done.3 = bf16[160,16,320]{2,0,1:T(8,128)(2,1)S(1)} async-done(((bf16[160,16,320]{2,0,1:T(8,128)(2,1)}), bf16[160,16,320]{2,0,1:T(8,128)(2,1)S(1)}, u32[]{:S(2)}, u32[]{:S(2)}) %all-to-all-start.3) | async-done | bytes 1638432 | tf_op jit(solution)/shard_map/all_to_all | solution.py:54
  139.1 10.7 %all-to-all-start.4 = ((bf16[16,320,864]{2,1,0:T(8,128)(2,1)}), bf16[16,320,864]{2,1,0:T(8,128)(2,1)}, u32[]{:S(2)}, u32[]{:S(2)}) async-start(bf16[16,320,864]{2,1,0:T(8,128)(2,1)} %bitcast.74), calls=%async_computation.4 | async-start | bytes 18350080 | tf_op jit(solution)/shard_map/all_to_all | solution.py:50
  149.8 12.7 %copy.80 = bf16[5120,864]{1,0:T(8,128)(2,1)} copy(bf16[5120,864]{0,1:T(8,128)(2,1)} %param.19) | data formatting | bytes 17694720 | tf_op args[6]
  162.5 151.6 %all-to-all-done.4 = bf16[16,320,864]{2,1,0:T(8,128)(2,1)} async-done(((bf16[16,320,864]{2,1,0:T(8,128)(2,1)}), bf16[16,320,864]{2,1,0:T(8,128)(2,1)}, u32[]{:S(2)}, u32[]{:S(2)}) %all-to-all-start.4) | async-done | bytes 8847392 | tf_op jit(solution)/shard_map/all_to_all | solution.py:50
  314.1 39.7 %all-to-all-start.5 = ((bf16[16,320,864]{2,1,0:T(8,128)(2,1)}), bf16[16,320,864]{2,1,0:T(8,128)(2,1)}, u32[]{:S(2)}, u32[]{:S(2)}) async-start(bf16[16,320,864]{2,1,0:T(8,128)(2,1)} %bitcast.75), calls=%async_computation.5 | async-start | bytes 18350080 | tf_op jit(solution)/shard_map/all_to_all | solution.py:51
  353.8 12.7 %copy.82 = bf16[864,5120]{0,1:T(8,128)(2,1)} copy(bf16[864,5120]{1,0:T(8,128)(2,1)} %param.20) | data formatting | bytes 17694720 | tf_op args[7]
  366.5 151.6 %all-to-all-done.5 = bf16[16,320,864]{2,1,0:T(8,128)(2,1)} async-done(((bf16[16,320,864]{2,1,0:T(8,128)(2,1)}), bf16[16,320,864]{2,1,0:T(8,128)(2,1)}, u32[]{:S(2)}, u32[]{:S(2)}) %all-to-all-start.5) | async-done | bytes 8847392 | tf_op jit(solution)/shard_map/all_to_all | solution.py:51
  518.1 40.0 %all-to-all-start.6 = ((bf16[864,16,320]{0,2,1:T(8,128)(2,1)}), bf16[864,16,320]{0,2,1:T(8,128)(2,1)}, u32[]{:S(2)}, u32[]{:S(2)}) async-start(bf16[864,16,320]{0,2,1:T(8,128)(2,1)} %bitcast.73), calls=%async_computation.6 | async-start | bytes 18350080 | tf_op jit(solution)/shard_map/all_to_all | solution.py:55
  558.6 1.6 abs_reduce_fusion.6
  560.3 1.6 abs_reduce_fusion.5
  563.5 5.9 abs_reduce_fusion.2
  569.5 5.8 abs_reduce_fusion.1
  575.4 2.3 abs_reduce_fusion
  577.7 201.4 %all-reduce.2 = (f32[1]{0:T(128)}, f32[1]{0:T(128)}, f32[1]{0:T(128)}, f32[1]{0:T(128)}, f32[1]{0:T(128)}, /*index=5*/f32[1]{0:T(128)}, f32[1]{0:T(128)}) all-reduce(f32[1]{0:T(128)} %bitcast, f32[1]{0:T(128)} %bitcast.1, f32[1]{0:T(128)} %bitcast.2, f32[1]{0:T(128)} %bitcast.3, ...), channel_id=1, replica_groups=mesh['fsdp'=16,'tp'=2] {'fsdp','tp'}, use_global_device_ids=true, to_apply=%region_1.0 | all-reduce | flops 7 | bytes 56 | tf_op jit(solution)/shard_map/pmax | solution.py:114
  781.0 4.5 stack.31
  785.7 31.4 %all-reduce.1 = f32[32]{0:T(128)S(1)} all-reduce(f32[32]{0:T(128)S(1)} %multiply_reduce_fusion), channel_id=3, replica_groups=mesh['fsdp'=16,'tp'=2] {'fsdp'}, use_global_device_ids=true, to_apply=%region_17.18.clone | all-reduce | flops 32 | bytes 256
  822.0 2.6 multiply_convert_fusion.4
  824.6 3.3 copy.84
  827.8 1.7 convolution_bitcast_fusion
  829.6 2.6 multiply_convert_fusion.3
  832.1 3.4 copy.87
  835.6 81.8 %all-reduce.5.cloned.1.call-done = f32[32,3584]{1,0:T(8,128)} async-done(((f32[32,3584]{1,0:T(8,128)}), f32[32,3584]{1,0:T(8,128)}) %all-reduce.5.cloned.1.call-update) | async-done | bytes 458768
  917.4 2.1 fusion.32
  919.5 1.6 fusion.28
  921.6 5.8 select_reduce_fusion
  927.9 4.7 fusion.20
  933.2 9.7 fusion
  943.0 12.4 %copy.79 = bf16[320,16,864]{2,1,0:T(8,128)(2,1)} copy(bf16[320,16,864]{2,0,1:T(8,128)(2,1)} %fusion) | data formatting | bytes 17694720 | tf_op jit(solution)/shard_map/convert_element_type | solution.py:28
  955.4 16.3 %convert_element_type.218 = bf16[320,13824]{1,0:T(8,128)(2,1)} reshape(bf16[320,16,864]{2,1,0:T(8,128)(2,1)} %copy.79) | data formatting | bytes 17694720 | tf_op jit(solution)/shard_map/convert_element_type | solution.py:28
  971.7 9.8 fusion.1
  981.5 12.4 %copy.81 = bf16[320,16,864]{2,1,0:T(8,128)(2,1)} copy(bf16[320,16,864]{2,0,1:T(8,128)(2,1)} %fusion.1) | data formatting | bytes 17694720 | tf_op jit(solution)/shard_map/convert_element_type | solution.py:28
  993.9 16.4 %convert_element_type.222 = bf16[320,13824]{1,0:T(8,128)(2,1)} reshape(bf16[320,16,864]{2,1,0:T(8,128)(2,1)} %copy.81) | data formatting | bytes 17694720 | tf_op jit(solution)/shard_map/convert_element_type | solution.py:28
  1010.3 9.8 fusion.2
  1020.1 12.4 %copy.83 = bf16[16,864,320]{1,0,2:T(8,128)(2,1)} copy(bf16[16,864,320]{1,2,0:T(8,128)(2,1)} %fusion.2) | data formatting | bytes 17694720 | tf_op jit(solution)/shard_map/convert_element_type | solution.py:28
  1032.5 16.1 %convert_element_type.226 = bf16[13824,320]{0,1:T(8,128)(2,1)} reshape(bf16[16,864,320]{1,0,2:T(8,128)(2,1)} %copy.83) | data formatting | bytes 17694720 | tf_op jit(solution)/shard_map/convert_element_type | solution.py:28
  (67 shorter events, 14.5 us)
Async XLA Ops:
  9.3 19.6 %all-to-all-start.1 = ((bf16[16,320,32]{1,2,0:T(8,128)(2,1)}), bf16[16,320,32]{1,2,0:T(8,128)(2,1)S(1)}, u32[]{:S(2)}, u32[]{:S(2)}) async-start(bf16[16,320,32]{1,2,0:T(8,128)(2,1)} %copy.69), calls=%async_computation.1 | async-start | bytes 786432 | tf_op jit(solution)/shard_map/all_to_all | solution.py:48
  28.9 0.7 copy-start.3
  29.6 15.7 %all-to-all-start.2 = ((bf16[16,320,32]{1,2,0:T(8,128)(2,1)}), bf16[16,320,32]{1,2,0:T(8,128)(2,1)S(1)}, u32[]{:S(2)}, u32[]{:S(2)}) async-start(bf16[16,320,32]{1,2,0:T(8,128)(2,1)} %copy.70), calls=%async_computation.2 | async-start | bytes 786432 | tf_op jit(solution)/shard_map/all_to_all | solution.py:49
  45.3 66.5 %copy-start.5 = (bf16[16,320,32]{1,2,0:T(8,128)(2,1)}, bf16[16,320,32]{1,2,0:T(8,128)(2,1)S(1)}, u32[]{:S(2)}) copy-start(bf16[16,320,32]{1,2,0:T(8,128)(2,1)S(1)} %all-to-all-done.2) | copy-start | bytes 983044
  45.3 43.1 %all-to-all-start = ((bf16[16,320,160]{1,2,0:T(8,128)(2,1)}), bf16[16,320,160]{1,2,0:T(8,128)(2,1)}, u32[]{:S(2)}, u32[]{:S(2)}) async-start(bf16[16,320,160]{1,2,0:T(8,128)(2,1)} %copy.68), calls=%async_computation | async-start | bytes 3932160 | tf_op jit(solution)/shard_map/all_to_all | solution.py:47
  88.4 49.4 %all-to-all-start.3 = ((bf16[160,16,320]{2,0,1:T(8,128)(2,1)}), bf16[160,16,320]{2,0,1:T(8,128)(2,1)S(1)}, u32[]{:S(2)}, u32[]{:S(2)}) async-start(bf16[160,16,320]{2,0,1:T(8,128)(2,1)} %copy.77), calls=%async_computation.3 | async-start | bytes 3932160 | tf_op jit(solution)/shard_map/all_to_all | solution.py:54
  137.8 1.3 copy-start
  139.1 175.0 %all-to-all-start.4 = ((bf16[16,320,864]{2,1,0:T(8,128)(2,1)}), bf16[16,320,864]{2,1,0:T(8,128)(2,1)}, u32[]{:S(2)}, u32[]{:S(2)}) async-start(bf16[16,320,864]{2,1,0:T(8,128)(2,1)} %bitcast.74), calls=%async_computation.4 | async-start | bytes 18350080 | tf_op jit(solution)/shard_map/all_to_all | solution.py:50
  314.1 204.0 %all-to-all-start.5 = ((bf16[16,320,864]{2,1,0:T(8,128)(2,1)}), bf16[16,320,864]{2,1,0:T(8,128)(2,1)}, u32[]{:S(2)}, u32[]{:S(2)}) async-start(bf16[16,320,864]{2,1,0:T(8,128)(2,1)} %bitcast.75), calls=%async_computation.5 | async-start | bytes 18350080 | tf_op jit(solution)/shard_map/all_to_all | solution.py:51
  518.1 43.8 %copy-start.1 = (bf16[5120,160]{0,1:T(8,128)(2,1)S(1)}, bf16[5120,160]{0,1:T(8,128)(2,1)}, u32[]{:S(2)}) copy-start(bf16[5120,160]{0,1:T(8,128)(2,1)} %param.14) | copy-start | bytes 4915204
  518.1 44.6 %copy-start.2 = (bf16[160,5120]{1,0:T(8,128)(2,1)S(1)}, bf16[160,5120]{1,0:T(8,128)(2,1)}, u32[]{:S(2)}) copy-start(bf16[160,5120]{1,0:T(8,128)(2,1)} %param.17) | copy-start | bytes 4915204
  518.1 492.2 %all-to-all-start.6 = ((bf16[864,16,320]{0,2,1:T(8,128)(2,1)}), bf16[864,16,320]{0,2,1:T(8,128)(2,1)}, u32[]{:S(2)}, u32[]{:S(2)}) async-start(bf16[864,16,320]{0,2,1:T(8,128)(2,1)} %bitcast.73), calls=%async_computation.6 | async-start | bytes 18350080 | tf_op jit(solution)/shard_map/all_to_all | solution.py:55
  558.1 359.3 %all-reduce.5.cloned.1.call-start = ((), (), s32[]{:S(2)}) async-start(), calls=%async_computation.7 | async-start | bytes 917504
  563.5 11.8 %slice-start = ((s8[8847360]{0:T(1024)(128)(4,1)}), s8[4194304]{0:T(1024)(128)(4,1)S(1)}, s32[]{:S(2)}) async-start(s8[8847360]{0:T(1024)(128)(4,1)} %bitcast.76), calls=%async_computation.8 | async-start | bytes 8388608
  563.5 11.8 %slice-start.1 = ((s8[8847360]{0:T(1024)(128)(4,1)}), s8[4194304]{0:T(1024)(128)(4,1)S(1)}, s32[]{:S(2)}) async-start(s8[8847360]{0:T(1024)(128)(4,1)} %bitcast.76), calls=%async_computation.9 | async-start | bytes 8388608
  569.5 5.9 slice-start.2
  569.5 210.2 %copy-start.9 = (s32[2]{0:T(128)S(1)}, s32[2]{0:T(128)}, u32[]{:S(2)}) copy-start(s32[2]{0:T(128)} %param.23) | copy-start | bytes 28
  569.5 210.3 %copy-start.10 = (u32[32]{0:T(128)S(1)}, u32[32]{0:T(128)}, u32[]{:S(2)}) copy-start(u32[32]{0:T(128)} %constant.29) | copy-start | bytes 388
  569.5 216.1 %copy-start.8 = (bf16[32,320]{1,0:T(8,128)(2,1)S(1)}, bf16[32,320]{1,0:T(8,128)(2,1)}, u32[]{:S(2)}) copy-start(bf16[32,320]{1,0:T(8,128)(2,1)} %param.13) | copy-start | bytes 61444
  569.5 247.6 %copy-start.7 = (f32[7,1024]{1,0:T(8,128)S(1)}, f32[7,1024]{1,0:T(8,128)}, u32[]{:S(2)}) copy-start(f32[7,1024]{1,0:T(8,128)} %param.21) | copy-start | bytes 86020
  569.5 249.3 %copy-start.4 = (bf16[16,320,32]{1,2,0:T(8,128)(2,1)S(1)}, bf16[16,320,32]{1,2,0:T(8,128)(2,1)}, u32[]{:S(2)}) copy-start(bf16[16,320,32]{1,2,0:T(8,128)(2,1)} %copy-done.3) | copy-start | bytes 983044
  569.5 251.0 %copy-start.6 = (bf16[16,320,32]{1,2,0:T(8,128)(2,1)S(1)}, bf16[16,320,32]{1,2,0:T(8,128)(2,1)}, u32[]{:S(2)}) copy-start(bf16[16,320,32]{1,2,0:T(8,128)(2,1)} %copy-done.5) | copy-start | bytes 983044
Sparse Core Ops, SparseCore 0:
  829.7 87.6 all-reduce.4
where the time goes:
time: 1060 us
  waiting for transfers between devices  462 us (44%)
  blocking collectives  233 us (22%)
  local copies, waits for them, and re-layouts  155 us (15%)
  starting transfers between devices  117 us (11%)
  other arithmetic  60.6 us (6%)
  between operations  15.9 us (2%)
  matrix products  12.2 us (1%)
    pmax x1, blocking collectives, per_device(): lax.pmax(largest(tensor), ('fsdp', 'tp'))  201 us
    all_to_all x1, waiting for transfers between devices, regroup(): lax.all_to_all(gate_part, 'fsdp', split_axis=0, concat_axis=1, tiled=True)  152 us
    all_to_all x1, waiting for transfers between devices, regroup(): lax.all_to_all(up_part, 'fsdp', split_axis=0, concat_axis=1, tiled=True)  152 us
    convert_element_type x6, local copies, waits for them, and re-layouts, quantize(): return (tensor.astype(jnp.float32) * factor).astype(jnp.bfloat16)  86.1 us
    unnamed x2, waiting for transfers between devices  81.9 us
    unnamed x36, local copies, waits for them, and re-layouts  49.3 us
    all_to_all x1, starting transfers between devices, regroup(): lax.all_to_all(down_part, 'fsdp', split_axis=1, concat_axis=0, tiled=True)  40 us
    all_to_all x1, starting transfers between devices, regroup(): lax.all_to_all(up_part, 'fsdp', split_axis=0, concat_axis=1, tiled=True)  39.7 us
  transfers between devices with their start and end apart: 8, of which 7 were waited for; matrix products, arithmetic and copies ran while one was open for 17% of the time, Pallas kernels for 0%

commit v1 on v0

--- a/solution.py
+++ b/solution.py
@@ -42,19 +42,38 @@
     )
 
 
-def regroup(query_part, key_part, value_part, output_part, gate_part, up_part, down_part):
-    columns = (
-        lax.all_to_all(query_part, "fsdp", split_axis=0, concat_axis=1, tiled=True),
-        lax.all_to_all(key_part, "fsdp", split_axis=0, concat_axis=1, tiled=True),
-        lax.all_to_all(value_part, "fsdp", split_axis=0, concat_axis=1, tiled=True),
-        lax.all_to_all(gate_part, "fsdp", split_axis=0, concat_axis=1, tiled=True),
-        lax.all_to_all(up_part, "fsdp", split_axis=0, concat_axis=1, tiled=True),
-    )
-    rowwise = (
-        lax.all_to_all(output_part, "fsdp", split_axis=1, concat_axis=0, tiled=True),
-        lax.all_to_all(down_part, "fsdp", split_axis=1, concat_axis=0, tiled=True),
-    )
-    return (columns[0], columns[1], columns[2], rowwise[0], columns[3], columns[4], rowwise[1])
+def after(tensor, *earlier):
+    return lax.optimization_barrier((tensor,) + earlier)[0]
+
+
+def exchange_columns(part, *earlier):
+    count = lax.axis_size("fsdp")
+    rows, width = part.shape
+    blocks = lax.optimization_barrier(part.reshape(count, rows // count, width))
+    return lax.all_to_all(
+        after(blocks, *earlier), "fsdp", split_axis=0, concat_axis=0, tiled=True
+    )
+
+
+def beside(blocks):
+    count, rows, width = blocks.shape
+    return blocks.transpose(1, 0, 2).reshape(rows, count * width)
+
+
+def exchange_rows(part, *earlier):
+    count = lax.axis_size("fsdp")
+    rows, width = part.shape
+    blocks = lax.optimization_barrier(
+        part.reshape(rows, count, width // count).transpose(1, 0, 2)
+    )
+    return lax.all_to_all(
+        after(blocks, *earlier), "fsdp", split_axis=0, concat_axis=0, tiled=True
+    )
+
+
+def below(blocks):
+    count, rows, width = blocks.shape
+    return blocks.reshape(count * rows, width)
 
 
 def attend(query, key_new, value_new, key_cache, value_cache, lengths):
@@ -111,29 +130,29 @@
         up_weight,
         down_weight,
     )
-    peaks = jnp.stack([lax.pmax(largest(tensor), ("fsdp", "tp")) for tensor in trainer])
+    wide_q, wide_k = query_weight.shape[1], key_weight.shape[1]
+    packed = exchange_columns(jnp.concatenate([query_weight, key_weight, value_weight], axis=1))
+    local = after(jnp.stack([largest(tensor) for tensor in trainer]), packed)
+    peaks = lax.pmax(local, ("fsdp", "tp"))
     factors, new_history = scaling(peaks, history, slot)
-    arrived = regroup(
-        query_weight, key_weight, value_weight, output_weight, gate_weight, up_weight, down_weight
-    )
-    rollout = tuple((quantize(arrived[number], factors[number]) for number in range(7)))
-    (
-        query_rollout,
-        key_rollout,
-        value_rollout,
-        output_rollout,
-        gate_rollout,
-        up_rollout,
-        down_rollout,
-    ) = rollout
+    gate_blocks = exchange_columns(gate_weight, peaks)
+    query_rollout = quantize(beside(packed[:, :, :wide_q]), factors[0])
+    key_rollout = quantize(beside(packed[:, :, wide_q : wide_q + wide_k]), factors[1])
+    value_rollout = quantize(beside(packed[:, :, wide_q + wide_k :]), factors[2])
     widened = hidden.astype(jnp.float32)
     squares = jnp.sum(widened * widened, axis=1)
     joined = jnp.concatenate([query_rollout, key_rollout, value_rollout], axis=1)
     partial_value = jnp.dot(hidden, joined, preferred_element_type=jnp.float32)
-    summed, total_sq = (
-        lax.psum_scatter(partial_value, "fsdp", scatter_dimension=0, tiled=True),
-        lax.psum_scatter(squares, "fsdp", scatter_dimension=0, tiled=True),
-    )
+    summed = lax.psum_scatter(
+        jnp.concatenate([partial_value, squares[:, None]], axis=1),
+        "fsdp",
+        scatter_dimension=0,
+        tiled=True,
+    )
+    up_blocks = exchange_columns(up_weight, gate_blocks, summed)
+    gate_rollout = quantize(beside(gate_blocks), factors[4])
+    total_sq = summed[:, -1]
+    summed = summed[:, :-1]
     inv_rms = lax.rsqrt(total_sq / D + norm_eps)[:, None]
     width_q = query_rollout.shape[1]
     width_k = key_rollout.shape[1]
@@ -146,6 +165,11 @@
     key_new = rotate(key_new.reshape(count_seq, -1, HEAD_DIM), lengths).astype(jnp.bfloat16)
     value_new = value_new.reshape(count_seq, -1, HEAD_DIM).astype(jnp.bfloat16)
     attention_out = attend(query, key_new, value_new, key_cache, value_cache, lengths)
+    down_arrived = exchange_rows(down_weight, up_blocks, gate_rollout, attention_out)
+    up_rollout = quantize(beside(up_blocks), factors[5])
+    output_arrived = exchange_rows(output_weight, down_arrived, up_rollout)
+    down_rollout = quantize(below(down_arrived), factors[6])
+    output_rollout = quantize(below(output_arrived), factors[3])
     return (
         attention_out,
         query_rollout,

time: 1060 us -> 918 us (0.87)
  blocking collectives: 233 us -> 48.8 us
  waiting for transfers between devices: 462 us -> 504 us
  starting transfers between devices: 117 us -> 97.3 us
    pmax x1, blocking collectives: 201 us -> 48.8 us  [per_device(): peaks = lax.pmax(local, ('fsdp', 'tp'))]
    unnamed x2, waiting for transfers between devices: 81.9 us -> 218 us
    all_to_all x7 -> x5, waiting for transfers between devices: 380 us -> 285 us  [the longest x3 164 us: exchange_columns(): lax.all_to_all(after(blocks, *earlier), 'fsdp', split_axis=0, concat_axis...]
    unnamed x1 -> x0, blocking collectives: 31.4 us -> none
    all_to_all x7 -> x5, starting transfers between devices: 116 us -> 97.1 us  [the longest x3 52.1 us: exchange_columns(): lax.all_to_all(after(blocks, *earlier), 'fsdp', split_axis=0, concat_axis...]
    all_to_all x8 -> x0, local copies, waits for them, and re-layouts: 14.3 us -> none  [the longest x2 5 us: regroup(): lax.all_to_all(output_part, 'fsdp', split_axis=1, concat_axis=0, tiled=True)]
    convert_element_type x6 -> x9, local copies, waits for them, and re-layouts: 86.1 us -> 93.2 us  [quantize(): return (tensor.astype(jnp.float32) * factor).astype(jnp.bfloat16)]
    convert_element_type x7 -> x6, other arithmetic: 35.8 us -> 38.2 us  [quantize(): return (tensor.astype(jnp.float32) * factor).astype(jnp.bfloat16)]
  transfers between devices with their start and end apart: 8 -> 6, of which waited for: 7 -> 4; matrix products, arithmetic and copies ran while one was open for 17% -> 25% of each run, Pallas kernels for 0% -> 0%
where the time goes in v1:
time: 918 us; the launch traced here: 907 us
  waiting for transfers between devices  504 us (55%)
  local copies, waits for them, and re-layouts  160 us (17%)
  starting transfers between devices  97.3 us (11%)
  other arithmetic  68.6 us (7%)
  blocking collectives  48.8 us (5%)
  between operations  16 us (2%)
  matrix products  13 us (1%)
    unnamed x2, waiting for transfers between devices  218 us
    all_to_all x3, waiting for transfers between devices, exchange_columns(): lax.all_to_all(after(blocks, *earlier), 'fsdp', split_axis=0, concat_axis...  164 us
    all_to_all x2, waiting for transfers between devices, exchange_rows(): lax.all_to_all(after(blocks, *earlier), 'fsdp', split_axis=0, concat_axis...  121 us
    convert_element_type x9, local copies, waits for them, and re-layouts, quantize(): return (tensor.astype(jnp.float32) * factor).astype(jnp.bfloat16)  93.2 us
    all_to_all x3, starting transfers between devices, exchange_columns(): lax.all_to_all(after(blocks, *earlier), 'fsdp', split_axis=0, concat_axis...  52.1 us
    pmax x1, blocking collectives, per_device(): peaks = lax.pmax(local, ('fsdp', 'tp'))  48.8 us
    unnamed x28, local copies, waits for them, and re-layouts  47.2 us
    all_to_all x2, starting transfers between devices, exchange_rows(): lax.all_to_all(after(blocks, *earlier), 'fsdp', split_axis=0, concat_axis...  44.9 us
  transfers between devices with their start and end apart: 6, of which 4 were waited for; matrix products, arithmetic and copies ran while one was open for 25% of the time, Pallas kernels for 0%

profile of v1, /device:TPU:0, one launch (start us, length us, event | category | flops | bytes accessed | tf_op | source)
XLA Modules:
  0.0 907.0 jit_solution(2341549663295404438)
XLA Ops:
  7.2 3.2 pad_maximum_fusion
  10.4 4.4 reshape.204
  14.8 3.8 copy.69
  18.6 7.4 all-to-all-start
  26.0 12.8 %copy.83 = bf16[5120,864]{1,0:T(8,128)(2,1)} copy(bf16[5120,864]{0,1:T(8,128)(2,1)} %param.18) | data formatting | bytes 17694720 | tf_op args[5]
  40.0 2.3 abs_reduce_fusion.4
  42.3 2.3 abs_reduce_fusion.3
  44.6 5.9 abs_reduce_fusion.2
  50.5 5.8 abs_reduce_fusion
  56.3 2.2 abs_reduce_fusion.1
  58.6 4.6 stack.31
  63.2 12.9 %all-to-all-done = bf16[16,320,224]{2,1,0:T(8,128)(2,1)S(1)} async-done(((bf16[16,320,224]{2,1,0:T(8,128)(2,1)}), bf16[16,320,224]{2,1,0:T(8,128)(2,1)S(1)}, u32[]{:S(2)}, u32[]{:S(2)}) %all-to-all-start) | async-done | bytes 2293792 | tf_op jit(solution)/shard_map/all_to_all | solution.py:53
  76.1 48.8 %pmax.7 = f32[7]{0:T(128)S(1)} all-reduce(f32[7]{0:T(128)S(1)} %stack.31), channel_id=1, replica_groups=mesh['fsdp'=16,'tp'=2] {'fsdp','tp'}, use_global_device_ids=true, to_apply=%region_7.0 | all-reduce | flops 7 | bytes 56 | tf_op jit(solution)/shard_map/pmax | solution.py:136
  124.8 5.0 all-to-all-start.1
  129.9 12.8 %copy.82 = bf16[5120,864]{1,0:T(8,128)(2,1)} copy(bf16[5120,864]{0,1:T(8,128)(2,1)} %param.19) | data formatting | bytes 17694720 | tf_op args[6]
  142.7 151.5 %all-to-all-done.1 = bf16[16,320,864]{2,1,0:T(8,128)(2,1)} async-done(((bf16[16,320,864]{2,1,0:T(8,128)(2,1)}), bf16[16,320,864]{2,1,0:T(8,128)(2,1)}, u32[]{:S(2)}, u32[]{:S(2)}) %all-to-all-start.1) | async-done | bytes 8847392 | tf_op jit(solution)/shard_map/all_to_all | solution.py:53
  294.1 39.7 %all-to-all-start.2 = ((bf16[16,320,864]{2,1,0:T(8,128)(2,1)}), bf16[16,320,864]{2,1,0:T(8,128)(2,1)}, u32[]{:S(2)}, u32[]{:S(2)}) async-start(bf16[16,320,864]{2,1,0:T(8,128)(2,1)} %bitcast.71), calls=%async_computation.2 | async-start | bytes 18350080 | tf_op jit(solution)/shard_map/all_to_all | solution.py:53
  336.5 2.7 fusion.16
  339.2 4.3 copy.70
  343.5 3.7 fusion.17
  347.2 1.6 copy.71
  348.9 1.6 copy.72
  350.5 2.5 convolution_bitcast_fusion
  353.9 12.7 %copy.81 = bf16[864,5120]{0,1:T(8,128)(2,1)} copy(bf16[864,5120]{1,0:T(8,128)(2,1)} %param.20) | data formatting | bytes 17694720 | tf_op args[7]
  368.0 218.3 %all-reduce.3.cloned.1.call-done = f32[32,3585]{1,0:T(8,128)} async-done(((f32[32,3585]{1,0:T(8,128)}), f32[32,3585]{1,0:T(8,128)}) %all-reduce.3.cloned.1.call-update) | async-done | bytes 458896
  587.2 2.2 fusion.34
  589.4 1.6 fusion.30
  591.5 5.8 select_reduce_fusion
  597.7 4.7 fusion.22
  603.1 9.7 %fusion = bf16[320,16,864]{2,0,1:T(8,128)(2,1)} fusion(bf16[16,320,864]{2,1,0:T(8,128)(2,1)} %all-to-all-done.1, f32[]{:T(128)} %bitcast.26), kind=kLoop, calls=%fused_computation.6 | loop fusion | flops 13271040 | bytes 17694724 | tf_op jit(solution)/shard_map/convert_element_type | solution.py:28
  612.8 12.4 %copy.84 = bf16[320,16,864]{2,1,0:T(8,128)(2,1)} copy(bf16[320,16,864]{2,0,1:T(8,128)(2,1)} %fusion) | data formatting | bytes 17694720 | tf_op jit(solution)/shard_map/convert_element_type | solution.py:28
  625.2 16.1 %convert_element_type.206 = bf16[320,13824]{1,0:T(8,128)(2,1)} reshape(bf16[320,16,864]{2,1,0:T(8,128)(2,1)} %copy.84) | data formatting | bytes 17694720 | tf_op jit(solution)/shard_map/convert_element_type | solution.py:28
  641.4 5.0 all-to-all-start.3
  646.4 3.3 reshape.210
  649.7 1.8 copy.110
  651.5 9.8 %fusion.1 = bf16[320,16,864]{2,0,1:T(8,128)(2,1)} fusion(bf16[16,320,864]{2,1,0:T(8,128)(2,1)} %all-to-all-done.2, f32[]{:T(128)} %bitcast.28), kind=kLoop, calls=%fused_computation.7 | loop fusion | flops 13271040 | bytes 17694724 | tf_op jit(solution)/shard_map/convert_element_type | solution.py:28
  661.3 12.4 %copy.85 = bf16[320,16,864]{2,1,0:T(8,128)(2,1)} copy(bf16[320,16,864]{2,0,1:T(8,128)(2,1)} %fusion.1) | data formatting | bytes 17694720 | tf_op jit(solution)/shard_map/convert_element_type | solution.py:28
  673.6 16.1 %convert_element_type.210 = bf16[320,13824]{1,0:T(8,128)(2,1)} reshape(bf16[320,16,864]{2,1,0:T(8,128)(2,1)} %copy.85) | data formatting | bytes 17694720 | tf_op jit(solution)/shard_map/convert_element_type | solution.py:28
  689.8 120.8 %all-to-all-done.3 = bf16[16,864,320]{1,2,0:T(8,128)(2,1)} async-done(((bf16[16,864,320]{1,2,0:T(8,128)(2,1)}), bf16[16,864,320]{1,2,0:T(8,128)(2,1)}, u32[]{:S(2)}, u32[]{:S(2)}) %all-to-all-start.3) | async-done | bytes 8847392 | tf_op jit(solution)/shard_map/all_to_all | solution.py:69
  810.6 39.9 %all-to-all-start.4 = ((bf16[16,160,320]{2,1,0:T(8,128)(2,1)}), bf16[16,160,320]{2,1,0:T(8,128)(2,1)}, u32[]{:S(2)}, u32[]{:S(2)}) async-start(bf16[16,160,320]{2,1,0:T(8,128)(2,1)} %bitcast.79), calls=%async_computation.4 | async-start | bytes 3932160 | tf_op jit(solution)/shard_map/all_to_all | solution.py:69
  850.5 0.9 copy.88
  851.4 3.2 copy.87
  854.7 0.9 copy.89
  855.6 9.8 %multiply_convert_fusion = bf16[16,864,320]{1,2,0:T(8,128)(2,1)} fusion(bf16[16,864,320]{1,2,0:T(8,128)(2,1)} %all-to-all-done.3, f32[]{:T(128)} %bitcast.32), kind=kLoop, calls=%fused_computation | loop fusion | flops 13271040 | bytes 17694724 | tf_op jit(solution)/shard_map/convert_element_type | solution.py:28
  865.4 12.4 %copy.86 = bf16[16,864,320]{1,0,2:T(8,128)(2,1)} copy(bf16[16,864,320]{1,2,0:T(8,128)(2,1)} %multiply_convert_fusion) | data formatting | bytes 17694720 | tf_op jit(solution)/shard_map/convert_element_type | solution.py:28
  877.8 16.1 %convert_element_type.216 = bf16[13824,320]{0,1:T(8,128)(2,1)} reshape(bf16[16,864,320]{1,0,2:T(8,128)(2,1)} %copy.86) | data formatting | bytes 17694720 | tf_op jit(solution)/shard_map/convert_element_type | solution.py:28
  894.0 2.5 multiply_convert_fusion.4
  896.4 3.3 copy.90
  (55 shorter events, 7.3 us)
Async XLA Ops:
  18.6 57.5 %all-to-all-start = ((bf16[16,320,224]{2,1,0:T(8,128)(2,1)}), bf16[16,320,224]{2,1,0:T(8,128)(2,1)S(1)}, u32[]{:S(2)}, u32[]{:S(2)}) async-start(bf16[16,320,224]{2,1,0:T(8,128)(2,1)} %copy.69), calls=%async_computation | async-start | bytes 5242880 | tf_op jit(solution)/shard_map/all_to_all | solution.py:53
  26.0 12.8 %copy-start.1 = (bf16[5120,32]{0,1:T(8,128)(2,1)S(1)}, bf16[5120,32]{0,1:T(8,128)(2,1)}, u32[]{:S(2)}) copy-start(bf16[5120,32]{0,1:T(8,128)(2,1)} %param.16) | copy-start | bytes 983044
  26.0 13.4 %copy-start.2 = (bf16[5120,32]{0,1:T(8,128)(2,1)S(1)}, bf16[5120,32]{0,1:T(8,128)(2,1)}, u32[]{:S(2)}) copy-start(bf16[5120,32]{0,1:T(8,128)(2,1)} %param.15) | copy-start | bytes 983044
  44.6 11.8 %slice-start = ((s8[8847360]{0:T(1024)(128)(4,1)}), s8[4194304]{0:T(1024)(128)(4,1)S(1)}, s32[]{:S(2)}) async-start(s8[8847360]{0:T(1024)(128)(4,1)} %bitcast.74), calls=%async_computation.6 | async-start | bytes 8388608
  44.6 11.8 %slice-start.1 = ((s8[8847360]{0:T(1024)(128)(4,1)}), s8[4194304]{0:T(1024)(128)(4,1)S(1)}, s32[]{:S(2)}) async-start(s8[8847360]{0:T(1024)(128)(4,1)} %bitcast.74), calls=%async_computation.7 | async-start | bytes 8388608
  50.5 5.8 slice-start.2
  124.8 169.3 %all-to-all-start.1 = ((bf16[16,320,864]{2,1,0:T(8,128)(2,1)}), bf16[16,320,864]{2,1,0:T(8,128)(2,1)}, u32[]{:S(2)}, u32[]{:S(2)}) async-start(bf16[16,320,864]{2,1,0:T(8,128)(2,1)} %bitcast.73), calls=%async_computation.1 | async-start | bytes 18350080 | tf_op jit(solution)/shard_map/all_to_all | solution.py:53
  142.7 192.1 %copy-start.4 = (bf16[32,320]{1,0:T(8,128)(2,1)S(1)}, bf16[32,320]{1,0:T(8,128)(2,1)}, u32[]{:S(2)}) copy-start(bf16[32,320]{1,0:T(8,128)(2,1)} %param.13) | copy-start | bytes 61444
  142.7 192.3 %copy-start.5 = (s32[2]{0:T(128)S(1)}, s32[2]{0:T(128)}, u32[]{:S(2)}) copy-start(s32[2]{0:T(128)} %param.23) | copy-start | bytes 28
  142.7 192.4 %copy-start.3 = (f32[7,1024]{1,0:T(8,128)S(1)}, f32[7,1024]{1,0:T(8,128)}, u32[]{:S(2)}) copy-start(f32[7,1024]{1,0:T(8,128)} %param.21) | copy-start | bytes 86020
  294.1 347.2 %all-to-all-start.2 = ((bf16[16,320,864]{2,1,0:T(8,128)(2,1)}), bf16[16,320,864]{2,1,0:T(8,128)(2,1)}, u32[]{:S(2)}, u32[]{:S(2)}) async-start(bf16[16,320,864]{2,1,0:T(8,128)(2,1)} %bitcast.71), calls=%async_computation.2 | async-start | bytes 18350080 | tf_op jit(solution)/shard_map/all_to_all | solution.py:53
  333.9 252.4 %all-reduce.3.cloned.1.call-start = ((), (), s32[]{:S(2)}) async-start(), calls=%async_computation.5 | async-start | bytes 950272
  353.9 12.7 %copy-start.6 = (u32[32]{0:T(128)S(1)}, u32[32]{0:T(128)}, u32[]{:S(2)}) copy-start(u32[32]{0:T(128)} %constant.29) | copy-start | bytes 388
  641.4 169.2 %all-to-all-start.3 = ((bf16[16,864,320]{1,2,0:T(8,128)(2,1)}), bf16[16,864,320]{1,2,0:T(8,128)(2,1)}, u32[]{:S(2)}, u32[]{:S(2)}) async-start(bf16[16,864,320]{1,2,0:T(8,128)(2,1)} %bitcast.72), calls=%async_computation.3 | async-start | bytes 18350080 | tf_op jit(solution)/shard_map/all_to_all | solution.py:69
  689.8 161.6 %copy-start = (bf16[320,16,160]{0,2,1:T(8,128)(2,1)S(1)}, bf16[320,16,160]{0,2,1:T(8,128)(2,1)}, u32[]{:S(2)}) copy-start(bf16[320,16,160]{0,2,1:T(8,128)(2,1)} %copy.70) | copy-start | bytes 4915204
  810.6 83.4 %all-to-all-start.4 = ((bf16[16,160,320]{2,1,0:T(8,128)(2,1)}), bf16[16,160,320]{2,1,0:T(8,128)(2,1)}, u32[]{:S(2)}, u32[]{:S(2)}) async-start(bf16[16,160,320]{2,1,0:T(8,128)(2,1)} %bitcast.79), calls=%async_computation.4 | async-start | bytes 3932160 | tf_op jit(solution)/shard_map/all_to_all | solution.py:69
Sparse Core Ops, SparseCore 0:
  354.0 232.2 all-reduce.2
